TPU v7x, 128 devices: a whole 4x4x4 slice. The times are simulated.
128 devices in a mesh: ma: 32 (over y, z, core), pb: 4 (over x).
Axes of the slice: x: 4, y: 4, z: 4, core: 2. Of those that a mesh axis runs over, the one named last changes fastest.
Arguments:
- coefs: float32 [512, 1056, 64], P('ma', 'pb'), may hold values from -6 to 6
- legendre: float32 [512, 1056, 4, 256], P('ma', None, 'pb'), may hold values from -0.25 to 0.25
- quad_weight: float32 [4, 256], P('pb'), may hold values from 0.3 to 3
- pair_of_slot: int32 [512], replicated, may hold values from 0 to 511, each once
- tracers: float32 [12, 2, 1024, 2048], P(None, None, ('ma', 'pb')), may hold values from 0 to 2
- heat_rate: float32 [12, 2], replicated, may hold values from -1.75 to 1.75
Outputs:
- spec_tendency: float32 [512, 1056, 64], P('ma', 'pb')
- tracers_new: float32 [12, 2, 1024, 2048], P(None, None, ('ma', 'pb'))
Inputs may be any that keep to these rules, and one draw needn't show every extreme that they name: Each pair number appears once; slot s holds the orders pair_of_slot[s] and 1023 - pair_of_slot[s].
All inputs are finite; a program needn't handle non-finite values.
Results may differ from a plain program's by a relative error of at most 0.00007.
Values sent between devices are 32-bit elements; how exact they have to be, the bound alone decides.
No kernel may reach another device: no remote copies, remote signals or barrier semaphores. Data moves between devices by JAX's collectives and lax.ppermute only.
A program may use at most 128 MiB of HBM per device.

v0:
```python
import math
import jax
import jax.numpy as jnp
from jax import lax
from jax.sharding import PartitionSpec as P

M = 1024
NLAT = 1024
NLON = 2048
LAYER_TOTAL = 8
NF = 4
NTR = 12
TLEV = 2
PAIRS = 512
COURANT = 0.15
DRAG_COEFFICIENT = 0.2
MOISTURE_SOURCE = 0.3
RAINFALL_FACTOR = 0.2
HIGHEST = lax.Precision.HIGHEST


def extended(array, sides, width):
    edges = {}
    for axis, dim in sides:
        count, length = (lax.axis_size(axis), array.shape[dim])
        up = [(i, (i + 1) % count) for i in range(count - 1)]
        last = lax.slice_in_dim(array, length - width, length, axis=dim)
        initial = lax.slice_in_dim(array, 0, width, axis=dim)
        edges[dim] = (
            lax.ppermute(last, axis, up),
            lax.ppermute(initial, axis, [(b, a) for a, b in up]),
        )
    done = []
    for _, dim in sides:
        low, high = edges[dim]
        around = [(width, width) if d in done else (0, 0) for d in range(array.ndim)]
        array = jnp.concatenate([jnp.pad(low, around), array, jnp.pad(high, around)], axis=dim)
        done.append(dim)
    return array


def order_tables(pair_of_slot):
    orders = jnp.stack([pair_of_slot, M - 1 - pair_of_slot], axis=1)
    points = jnp.arange(NLON, dtype=jnp.int32)
    phases = orders[:, :, None] * points[None, None, :] % NLON
    angles = phases.astype(jnp.float32) * (2.0 * math.pi / NLON)
    factor = 1.0 / math.sqrt(NLON)
    fourier_table = jnp.stack([jnp.cos(angles) * factor, -jnp.sin(angles) * factor], axis=0)
    weights = jnp.where(orders == 0, 1.0, 2.0).astype(jnp.float32)
    return (fourier_table, weights)


def row_masks(pair_ids, row_count):
    row_ids = jnp.arange(row_count, dtype=jnp.int32)
    bounds = (M - pair_ids)[:, None]
    low_rows = row_ids[None, :] < bounds
    high_rows = (row_ids[None, :] >= bounds) & (row_ids[None, :] <= M)
    return (low_rows, high_rows)


def advect(padded, zonal_wind, southward, first_row):
    middle = padded[:, :, 1:-1, :]
    east_face = 0.5 * (zonal_wind + jnp.roll(zonal_wind, -1, axis=-1))
    flux_east = jnp.maximum(east_face, 0.0) * middle + jnp.minimum(east_face, 0.0) * jnp.roll(
        middle, -1, axis=-1
    )
    across = 0.5 * (southward[:, :-1, :] + southward[:, 1:, :])
    flux_south = (
        jnp.maximum(across, 0.0) * padded[:, :, :-1, :]
        + jnp.minimum(across, 0.0) * padded[:, :, 1:, :]
    )
    upper_row = first_row - 1 + jnp.arange(across.shape[1], dtype=jnp.int32)
    inside = (upper_row >= 0) & (upper_row <= NLAT - 2)
    flux_south = jnp.where(inside[None, None, :, None], flux_south, 0.0)
    change = (
        flux_east
        - jnp.roll(flux_east, 1, axis=-1)
        + (flux_south[:, :, 1:, :] - flux_south[:, :, :-1, :])
    )
    return -COURANT * change


def shards(coefs, legendre, quad_weight, pair_of_slot, tracers, heat_rate):
    slot_count = coefs.shape[0]
    row_block = coefs.shape[1]
    columns = coefs.shape[2]
    quarter = legendre.shape[3]
    legendre_rows = legendre.reshape(slot_count, legendre.shape[1], quarter)
    own_pairs = lax.dynamic_slice_in_dim(
        pair_of_slot, lax.axis_index("ma") * slot_count, slot_count, 0
    )
    row_piece = lax.all_gather(coefs, "pb", axis=1, tiled=True)
    row_count = row_piece.shape[1]
    low_rows, high_rows = row_masks(own_pairs, row_count)
    masked = jnp.concatenate(
        [
            jnp.where(low_rows[:, :, None], row_piece, 0.0),
            jnp.where(high_rows[:, :, None], row_piece, 0.0),
        ],
        axis=2,
    )
    table_rows = legendre_rows
    legendre_sum = jnp.einsum("srl,src->slc", table_rows, masked, precision=HIGHEST)
    bands = lax.all_to_all(legendre_sum, "ma", split_axis=1, concat_axis=0, tiled=True)
    band_rows = bands.shape[1]
    fourier_table, weights = order_tables(pair_of_slot)
    spectral = (
        bands.reshape(PAIRS, band_rows, 2, 2, NF * LAYER_TOTAL) * weights[:, None, :, None, None]
    )
    physical_space_field = jnp.einsum("sjhpc,pshi->jci", spectral, fourier_table, precision=HIGHEST)
    zonal_wind = jnp.transpose(physical_space_field[:, 0:TLEV, :], (1, 0, 2))
    southward = -jnp.transpose(
        physical_space_field[:, LAYER_TOTAL : LAYER_TOTAL + TLEV, :], (1, 0, 2)
    )
    first_row = lax.axis_index(("ma", "pb")) * band_rows
    stacked = jnp.concatenate([tracers, zonal_wind[None], southward[None]], axis=0)
    widened = extended(stacked, ((("ma", "pb"), 2),), 3)
    anchor = widened[:NTR]
    zonal_ext = widened[NTR]
    south_ext = widened[NTR + 1]
    first_section = anchor[:, :, 1:-1] + advect(
        anchor, zonal_ext[:, 1:-1], south_ext, first_row - 2
    )
    second = 0.75 * anchor[:, :, 2:-2] + 0.25 * (
        first_section[:, :, 1:-1]
        + advect(first_section, zonal_ext[:, 2:-2], south_ext[:, 1:-1], first_row - 1)
    )
    new_tracers = tracers / 3.0 + 2.0 / 3.0 * (
        second[:, :, 1:-1] + advect(second, zonal_ext[:, 3:-3], south_ext[:, 2:-2], first_row)
    )
    heating = jnp.einsum("kl,klji->jli", heat_rate, new_tracers, precision=HIGHEST)
    eastward_finished = physical_space_field[:, 0:LAYER_TOTAL]
    northward_velocity = physical_space_field[:, LAYER_TOTAL : 2 * LAYER_TOTAL]
    thermal_state = physical_space_field[:, 2 * LAYER_TOTAL : 3 * LAYER_TOTAL]
    vapour_mixing_share = physical_space_field[:, 3 * LAYER_TOTAL : 4 * LAYER_TOTAL]
    flow_speed_norm = jnp.sqrt(
        eastward_finished * eastward_finished + northward_velocity * northward_velocity + 1.0
    )
    warming_finished = jnp.pad(heating, ((0, 0), (0, LAYER_TOTAL - TLEV), (0, 0)))
    rate_of_change_field = jnp.concatenate(
        [
            -DRAG_COEFFICIENT * flow_speed_norm * eastward_finished,
            -DRAG_COEFFICIENT * flow_speed_norm * northward_velocity,
            warming_finished - MOISTURE_SOURCE * thermal_state * vapour_mixing_share,
            MOISTURE_SOURCE * thermal_state * vapour_mixing_share
            - RAINFALL_FACTOR * flow_speed_norm * vapour_mixing_share,
        ],
        axis=1,
    )
    fourier = jnp.einsum(
        "jci,pshi->sjhpc", rate_of_change_field, fourier_table, precision=HIGHEST
    ).reshape(PAIRS, band_rows, 2 * columns)
    by_orders = lax.all_to_all(fourier, "ma", split_axis=0, concat_axis=1, tiled=True)
    weighted = by_orders * quad_weight.reshape(quarter)[None, :, None]
    table_rows = legendre_rows
    row_sums = jnp.einsum("srl,slc->rsc", table_rows, weighted, precision=HIGHEST)
    low_rows, high_rows = row_masks(own_pairs, row_block * lax.axis_size("pb"))
    summed = lax.psum_scatter(
        jnp.where(low_rows.T[:, :, None], row_sums[:, :, :columns], 0.0)
        + jnp.where(high_rows.T[:, :, None], row_sums[:, :, columns:], 0.0),
        "pb",
        scatter_dimension=0,
        tiled=True,
    )
    return (jnp.transpose(summed, (1, 0, 2)), new_tracers)


def solution(mesh):
    in_specs = (
        P("ma", "pb", None),
        P("ma", None, "pb", None),
        P("pb", None),
        P(),
        P(None, None, ("ma", "pb"), None),
        P(),
    )
    out_specs = (P("ma", "pb", None), P(None, None, ("ma", "pb"), None))
    return jax.shard_map(shards, mesh=mesh, in_specs=in_specs, out_specs=out_specs, check_vma=False)
```

profile of v0, /device:TPU:1, one launch (start us, length us, event | category | flops | bytes accessed | tf_op | source)
XLA Modules:
  0.0 511.0 jit_solution(13479577784716797474)
XLA Ops:
  7.2 2.9 copy.83
  10.3 0.6 copy-done.7
  11.0 87.7 %all-gather.2.cloned.1.call-done = f32[16,1056,64]{2,1,0:T(8,128)} async-done(((f32[16,264,64]{2,1,0:T(8,128)}), f32[16,1056,64]{2,1,0:T(8,128)}) %all-gather.2.cloned.1.call-update) | async-done | bytes 4325392 | tf_op jit(solution)/shard_map/all_gather | solution.py:92
  98.6 10.0 %broadcast_select_fusion.1 = (f32[16,1056,64]{2,1,0:T(8,128)}, f32[16,1056,64]{2,1,0:T(8,128)}) fusion(f32[16,1056,64]{2,1,0:T(8,128)} %all-gather.2.cloned.1.call-done, pred[16,1056]{1,0:T(8,128)(4,1)S(1)} %get-tuple-element.42, pred[16,1056]{1,0:T(8,128)(4,1)S(1)} %get-tuple-element.43), kind=kLoop, calls=%fused_computation.30 | loop fusion | flops 2162688 | bytes 13009920 | tf_op jit(solution)/shard_map/jit(_where)/select_n | solution.py:97
  108.7 26.4 %fusion.60 = f32[16,256,128]{1,2,0:T(8,128)S(1)} fusion(f32[16,1056,1,256]{3,2,1,0:T(1,128)} %param.7, f32[16,1056,64]{2,1,0:T(8,128)} %get-tuple-element.19, f32[16,1056,64]{2,1,0:T(8,128)} %get-tuple-element.18), kind=kOutput, calls=%fused_computation.87 | convolution fusion | flops 6645940224 | bytes 28049408 | tf_op jit(solution)/shard_map/srl,src->slc/dot_general | solution.py:103
  135.1 2.0 copy.84
  137.1 7.9 %all-to-all-start = ((f32[16,256,128]{2,0,1:T(8,128)}), f32[16,256,128]{2,0,1:T(8,128)}, u32[]{:S(2)}, u32[]{:S(2)}) async-start(f32[16,256,128]{2,0,1:T(8,128)} %copy.84), calls=%async_computation | async-start | bytes 4194304 | tf_op jit(solution)/shard_map/all_to_all | solution.py:104
  145.2 2.3 copy.89
  147.6 37.4 %cosine_multiply_fusion = (f32[1,512,2,2048]{3,1,0,2:T(8,128)}, f32[1,512,2,2048]{3,1,0,2:T(8,128)}) fusion(s32[512,2]{0,1:T(2,128)S(1)} %pad_add_fusion), kind=kLoop, calls=%fused_computation.24 | loop fusion | flops 35651584 | bytes 16781312 | tf_op jit(solution)/shard_map/mul | solution.py:48
  184.9 3.8 copy.86
  188.7 10.0 %reshape.233 = f32[512,8,2,2,32]{4,3,2,1,0:T(2,128)} reshape(f32[32,16,8,128]{3,2,1,0:T(8,128)} %copy.86) | data formatting | bytes 4194304 | tf_op jit(solution)/shard_map/reshape | solution.py:108
  198.7 5.6 %broadcast_multiply_fusion = f32[512,8,2,2,32]{4,3,2,1,0:T(2,128)S(1)} fusion(f32[512,8,2,2,32]{4,3,2,1,0:T(2,128)} %reshape.233, f32[512,2]{1,0:T(8,128)S(1)} %copy.87), kind=kLoop, calls=%fused_computation.31 | loop fusion | flops 524288 | bytes 4198400 | tf_op jit(solution)/shard_map/mul | solution.py:108
  204.4 73.6 %fusion.33 = f32[8,32,2048]{2,1,0:T(8,128)S(1)} fusion(f32[512,8,2,2,32]{4,3,2,1,0:T(2,128)S(1)} %broadcast_multiply_fusion, f32[1,512,2,2048]{3,1,0,2:T(8,128)} %get-tuple-element.39, f32[1,512,2,2048]{3,1,0,2:T(8,128)} %get-tuple-element.38), kind=kOutput, calls=%fused_computation.53 | convolution fusion | flops 12889096192 | bytes 20971520 | tf_op jit(solution)/shard_map/sjhpc,pshi->jci/dot_general | solution.py:110
  278.4 1.4 pad_maximum_fusion.7
  279.8 3.1 collective-permute-start
  282.9 3.7 collective-permute-start.1
  286.6 0.6 compare_and_fusion.1
  287.7 14.4 %collective-permute-done = f32[14,2,3,2048]{3,0,2,1:T(8,128)S(1)} collective-permute-done((f32[14,2,3,2048]{3,0,2,1:T(8,128)}, f32[14,2,3,2048]{3,0,2,1:T(8,128)S(1)}, u32[]{:S(2)}, u32[]{:S(2)}) %collective-permute-start) | collective-permute-done | bytes 688160 | tf_op jit(solution)/shard_map/ppermute | solution.py:30
  302.2 1.4 collective-permute-done.1
  303.6 1.8 pad_maximum_fusion.9
  305.8 0.9 slice.298
  306.6 0.7 slice.297
  307.3 0.6 slice.299
  309.0 1.6 pad_maximum_fusion
  310.7 0.9 slice.273
  311.5 2.4 fusion.30
  314.6 0.9 fusion.24
  315.5 1.5 fusion.27
  317.0 0.7 slice.286
  318.5 0.9 fusion.41
  319.7 0.7 fusion.32
  320.4 1.6 fusion.40
  322.1 0.6 slice.300
  323.2 0.6 fusion.49
  324.1 0.6 fusion.43
  324.7 0.8 copy-done.1
  325.5 2.2 fusion.48
  327.7 1.6 fusion.80
  329.9 17.4 %fusion.57 = f32[512,8,2,2,32]{0,4,1,2,3:T(8,128)S(1)} fusion(f32[8,8,2048]{2,1,0:T(8,128)S(1)} %get-tuple-element.25, f32[8,8,2048]{2,1,0:T(8,128)S(1)} %get-tuple-element.26, f32[8,8,2048]{2,1,0:T(8,128)S(1)} %get-tuple-element.27, f32[8,8,2048]{2,1,0:T(8,128)S(1)} %get-tuple-element.24, f32[1,512,2,2048]{3,1,0,2:T(8,128)} %get-tuple-element.39, ...), kind=kOutput, calls=%fused_computation.86 | convolution fusion | flops 12890669056 | bytes 20971520 | tf_op jit(solution)/shard_map/jci,pshi->sjhpc/dot_general | solution.py:150
  347.2 1.6 copy.109
  348.8 2.9 copy.110
  351.8 8.7 %all-to-all-start.1 = ((f32[512,8,128]{2,1,0:T(8,128)}), f32[512,8,128]{2,1,0:T(8,128)}, u32[]{:S(2)}, u32[]{:S(2)}) async-start(f32[512,8,128]{2,1,0:T(8,128)} %copy.110), calls=%async_computation.1 | async-start | bytes 4194304 | tf_op jit(solution)/shard_map/all_to_all | solution.py:153
  360.6 28.2 %all-to-all-done.1 = f32[512,8,128]{2,1,0:T(8,128)} async-done(((f32[512,8,128]{2,1,0:T(8,128)}), f32[512,8,128]{2,1,0:T(8,128)}, u32[]{:S(2)}, u32[]{:S(2)}) %all-to-all-start.1) | async-done | bytes 2097184 | tf_op jit(solution)/shard_map/all_to_all | solution.py:153
  388.8 21.9 %fusion.20 = f32[1056,16,128]{2,0,1:T(8,128)S(1)} fusion(f32[16,1056,1,256]{3,2,1,0:T(1,128)} %param.7, f32[16,32,8,128]{3,2,0,1:T(8,128)} %bitcast.26, f32[256]{0:T(256)S(1)} %bitcast.86), kind=kOutput, calls=%fused_computation.28 | convolution fusion | flops 6644301824 | bytes 28050432 | tf_op jit(solution)/shard_map/srl,slc->rsc/dot_general | solution.py:156
  410.7 9.5 %fusion.8 = f32[1056,16,64]{2,0,1:T(8,128)} fusion(f32[1056,16,128]{2,0,1:T(8,128)S(1)} %fusion.20, pred[1056,16]{0,1:T(8,128)(4,1)S(1)} %get-tuple-element.41, pred[1056,16]{0,1:T(8,128)(4,1)S(1)} %get-tuple-element.40), kind=kLoop, calls=%fused_computation.13 | loop fusion | flops 3244032 | bytes 13009920 | tf_op jit(solution)/shard_map/add | solution.py:159
  420.2 2.1 copy.113
  422.3 78.4 %reduce-scatter.2.cloned.1.call-done = f32[264,16,64]{2,0,1:T(8,128)} async-done(((f32[1056,16,64]{2,0,1:T(8,128)}), f32[264,16,64]{2,0,1:T(8,128)}) %reduce-scatter.2.cloned.1.call-update) | async-done | bytes 1081360 | tf_op jit(solution)/shard_map/reduce_scatter | solution.py:158
  500.6 3.0 copy.112
  (83 shorter events, 5.7 us)
Async XLA Ops:
  7.2 320.5 %copy-start = (f32[12,2]{0,1:T(2,128)S(1)}, f32[12,2]{0,1:T(2,128)}, u32[]{:S(2)}) copy-start(f32[12,2]{0,1:T(2,128)} %param.11) | copy-start | bytes 292
  7.2 3.0 copy-start.9
  7.2 91.5 %all-gather.2.cloned.1.call-start = ((), (), s32[]{:S(2)}) async-start(), calls=%async_computation.3 | async-start | bytes 10813440 | tf_op jit(solution)/shard_map/all_gather | solution.py:92
  10.3 98.4 %copy-start.10 = (s32[16]{0:T(128)}, s32[16]{0:T(128)S(1)}, u32[]{:S(2)}) copy-start(s32[16]{0:T(128)S(1)} %dynamic-slice_subtract_fusion) | copy-start | bytes 196
  10.3 0.6 copy-start.7
  137.1 47.8 %all-to-all-start = ((f32[16,256,128]{2,0,1:T(8,128)}), f32[16,256,128]{2,0,1:T(8,128)}, u32[]{:S(2)}, u32[]{:S(2)}) async-start(f32[16,256,128]{2,0,1:T(8,128)} %copy.84), calls=%async_computation | async-start | bytes 4194304 | tf_op jit(solution)/shard_map/all_to_all | solution.py:104
  278.0 1.8 copy-start.2
  279.8 22.4 %collective-permute-start = (f32[14,2,3,2048]{3,0,2,1:T(8,128)}, f32[14,2,3,2048]{3,0,2,1:T(8,128)S(1)}, u32[]{:S(2)}, u32[]{:S(2)}) collective-permute-start(f32[14,2,3,2048]{3,0,2,1:T(8,128)} %get-tuple-element.22), channel_id=1, source_target_pairs={{0,1},{1,2},{2,3},{3,4},{4,5},{5,6},{6,7},{7,8},{8,9},{9,10},{10,1... | collective-permute-start | bytes 2064392 | tf_op jit(solution)/shard_map/ppermute | solution.py:30
  282.9 20.7 %collective-permute-start.1 = (f32[14,2,3,2048]{3,0,2,1:T(8,128)}, f32[14,2,3,2048]{3,0,2,1:T(8,128)}, u32[]{:S(2)}, u32[]{:S(2)}) collective-permute-start(f32[14,2,3,2048]{3,0,2,1:T(8,128)} %get-tuple-element.23), channel_id=1, source_target_pairs={{1,0},{2,1},{3,2},{4,3},{5,4},{6,5},{7,6},{8,7},{9,8},{10,9},{11,1... | collective-permute-start | bytes 2064392 | tf_op jit(solution)/shard_map/ppermute | solution.py:31
  318.5 1.2 copy-start.14
  322.0 0.9 copy-start.4
  322.0 1.0 copy-start.6
  322.1 1.0 copy-start.5
  323.2 0.9 copy-start.13
  324.1 1.4 copy-start.1
  324.7 5.1 %slice-start = ((s8[8388608]{0:T(1024)(128)(4,1)}), s8[4194304]{0:T(1024)(128)(4,1)S(1)}, s32[]{:S(2)}) async-start(s8[8388608]{0:T(1024)(128)(4,1)} %bitcast.77), calls=%async_computation.5 | async-start | bytes 8388608
  325.5 4.3 slice-start.1
  327.7 1.8 copy-start.3
  351.7 8.7 %copy-start.8 = (pred[1056]{0:T(1024)(128)(4,1)S(1)}, pred[1056]{0:T(1024)(128)(4,1)}, u32[]{:S(2)}) copy-start(pred[1056]{0:T(1024)(128)(4,1)} %copy-done.7) | copy-start | bytes 3172
  351.7 8.8 %copy-start.11 = (s32[16]{0:T(128)S(1)}, s32[16]{0:T(128)}, u32[]{:S(2)}) copy-start(s32[16]{0:T(128)} %copy-done.10) | copy-start | bytes 196
  351.8 37.1 %copy-start.12 = (f32[1,256]{1,0:T(1,128)S(1)}, f32[1,256]{1,0:T(1,128)}, u32[]{:S(2)}) copy-start(f32[1,256]{1,0:T(1,128)} %param.8) | copy-start | bytes 3076
  351.8 37.1 %all-to-all-start.1 = ((f32[512,8,128]{2,1,0:T(8,128)}), f32[512,8,128]{2,1,0:T(8,128)}, u32[]{:S(2)}, u32[]{:S(2)}) async-start(f32[512,8,128]{2,1,0:T(8,128)} %copy.110), calls=%async_computation.1 | async-start | bytes 4194304 | tf_op jit(solution)/shard_map/all_to_all | solution.py:153
  360.4 140.2 %reduce-scatter.2.cloned.1.call-start = ((), (), s32[]{:S(2)}) async-start(), calls=%async_computation.4 | async-start | bytes 10813440 | tf_op jit(solution)/shard_map/reduce_scatter | solution.py:158
Sparse Core Ops, SparseCore 0:
  10.3 88.2 all-gather.1
  420.3 80.2 reduce-scatter.1
where the time goes:
time: 520 us; the launch traced here: 511 us
  waiting for transfers between devices  210 us (40%)
  matrix products  141 us (27%)
  other arithmetic  81.8 us (16%)
  local copies, waits for them, and re-layouts  39.5 us (8%)
  starting transfers between devices  23.4 us (4%)
  between operations  15.1 us (3%)
    all_gather x1, waiting for transfers between devices, shards(): row_piece = lax.all_gather(coefs, 'pb', axis=1, tiled=True)  87.7 us
    reduce_scatter x1, waiting for transfers between devices, shards(): lax.psum_scatter(jnp.where(low_rows.T[:, :, None], row_sums[:, :, :column...  78.4 us
    dot_general x1, matrix products, shards(): jnp.einsum('sjhpc,pshi->jci', spectral, fourier_table, precision=HIGHEST)  73.6 us
    mul x1, other arithmetic, order_tables(): jnp.cos(angles) * factor  37.4 us
    all_to_all x1, waiting for transfers between devices, shards(): lax.all_to_all(fourier, 'ma', split_axis=0, concat_axis=1, tiled=True)  28.2 us
    dot_general x1, matrix products, shards(): jnp.einsum('srl,src->slc', table_rows, masked, precision=HIGHEST)  26.4 us
    dot_general x1, matrix products, shards(): jnp.einsum('srl,slc->rsc', table_rows, weighted, precision=HIGHEST)  21.9 us
    dot_general x1, matrix products, shards(): jnp.einsum('jci,pshi->sjhpc', rate_of_change_field, fourier_table, precis...  17.4 us
  transfers between devices with their start and end apart: 6, of which 5 were waited for; matrix products, arithmetic and copies ran while one was open for 8% of the time, Pallas kernels for 0%

commit v1 on v0

--- a/solution.py
+++ b/solution.py
@@ -89,7 +89,7 @@
     own_pairs = lax.dynamic_slice_in_dim(
         pair_of_slot, lax.axis_index("ma") * slot_count, slot_count, 0
     )
-    row_piece = lax.all_gather(coefs, "pb", axis=1, tiled=True)
+    row_piece = jnp.concatenate(lax.all_gather(coefs, "pb"), axis=1)
     row_count = row_piece.shape[1]
     low_rows, high_rows = row_masks(own_pairs, row_count)
     masked = jnp.concatenate(

time: 520 us -> 509 us (0.979)
  waiting for transfers between devices: 210 us -> 192 us
  local copies, waits for them, and re-layouts: 39.5 us -> 45.8 us
    all_gather x1, waiting for transfers between devices: 87.7 us -> 68.5 us  [shards(): row_piece = jnp.concatenate(lax.all_gather(coefs, 'pb'), axis=1)]
    all_gather x0 -> x1, local copies, waits for them, and re-layouts: none -> 8.8 us  [shards(): row_piece = jnp.concatenate(lax.all_gather(coefs, 'pb'), axis=1)]
    unnamed x40 -> x39, local copies, waits for them, and re-layouts: 12 us -> 9.51 us
  transfers between devices with their start and end apart: 6 -> 6, of which waited for: 5 -> 5; matrix products, arithmetic and copies ran while one was open for 8% -> 9% of each run, Pallas kernels for 0% -> 0%
where the time goes in v1:
time: 509 us; the launch traced here: 500 us
  waiting for transfers between devices  192 us (38%)
  matrix products  141 us (28%)
  other arithmetic  82.5 us (16%)
  local copies, waits for them, and re-layouts  45.8 us (9%)
  starting transfers between devices  23.8 us (5%)
  between operations  15.1 us (3%)
    reduce_scatter x1, waiting for transfers between devices, shards(): lax.psum_scatter(jnp.where(low_rows.T[:, :, None], row_sums[:, :, :column...  78.7 us
    dot_general x1, matrix products, shards(): jnp.einsum('sjhpc,pshi->jci', spectral, fourier_table, precision=HIGHEST)  73.6 us
    all_gather x1, waiting for transfers between devices, shards(): row_piece = jnp.concatenate(lax.all_gather(coefs, 'pb'), axis=1)  68.5 us
    mul x1, other arithmetic, order_tables(): jnp.cos(angles) * factor  37.4 us
    all_to_all x1, waiting for transfers between devices, shards(): lax.all_to_all(fourier, 'ma', split_axis=0, concat_axis=1, tiled=True)  28.2 us
    dot_general x1, matrix products, shards(): jnp.einsum('srl,src->slc', table_rows, masked, precision=HIGHEST)  26.4 us
    dot_general x1, matrix products, shards(): jnp.einsum('srl,slc->rsc', table_rows, weighted, precision=HIGHEST)  21.9 us
    dot_general x1, matrix products, shards(): jnp.einsum('jci,pshi->sjhpc', rate_of_change_field, fourier_table, precis...  17.4 us
  transfers between devices with their start and end apart: 6, of which 5 were waited for; matrix products, arithmetic and copies ran while one was open for 9% of the time, Pallas kernels for 0%

profile of v1, /device:TPU:1, one launch (start us, length us, event | category | flops | bytes accessed | tf_op | source)
XLA Modules:
  0.0 499.8 jit_solution(7767941320369879879)
XLA Ops:
  7.2 0.7 all-gather.3.cloned.1.call-update
  7.9 0.8 dynamic-slice_subtract_fusion
  9.8 68.5 %all-gather.3.cloned.1.call-done = f32[64,264,64]{1,2,0:T(8,128)} async-done(((f32[16,264,64]{1,2,0:T(8,128)}), f32[64,264,64]{1,2,0:T(8,128)}) %all-gather.3.cloned.1.call-update) | async-done | bytes 4325392 | tf_op jit(solution)/shard_map/all_gather | solution.py:92
  78.3 8.8 %copy.83 = f32[4,16,264,64]{3,2,0,1:T(8,128)} copy(f32[4,16,264,64]{2,3,1,0:T(8,128)} %bitcast.86) | data formatting | bytes 8650752 | tf_op jit(solution)/shard_map/all_gather | solution.py:92
  87.1 10.0 %bitcast_select_fusion.1 = (f32[16,1056,64]{2,1,0:T(8,128)}, f32[16,1056,64]{2,1,0:T(8,128)}) fusion(f32[4,16,264,64]{3,2,0,1:T(8,128)} %copy.83, pred[16,1056]{1,0:T(8,128)(4,1)S(1)} %get-tuple-element.42, pred[16,1056]{1,0:T(8,128)(4,1)S(1)} %get-tuple-element.43), kind=kLoop, calls=%fused_computation.19 | loop fusion | flops 2162688 | bytes 13009920 | tf_op jit(solution)/shard_map/jit(_where)/select_n | solution.py:97
  97.1 26.4 %fusion.60 = f32[16,256,128]{1,2,0:T(8,128)S(1)} fusion(f32[16,1056,1,256]{3,2,1,0:T(1,128)} %param.7, f32[16,1056,64]{2,1,0:T(8,128)} %get-tuple-element.19, f32[16,1056,64]{2,1,0:T(8,128)} %get-tuple-element.18), kind=kOutput, calls=%fused_computation.87 | convolution fusion | flops 6645940224 | bytes 28049408 | tf_op jit(solution)/shard_map/srl,src->slc/dot_general | solution.py:103
  123.6 2.0 copy.84
  125.5 8.3 %all-to-all-start = ((f32[16,256,128]{2,0,1:T(8,128)}), f32[16,256,128]{2,0,1:T(8,128)}, u32[]{:S(2)}, u32[]{:S(2)}) async-start(f32[16,256,128]{2,0,1:T(8,128)} %copy.84), calls=%async_computation | async-start | bytes 4194304 | tf_op jit(solution)/shard_map/all_to_all | solution.py:104
  134.0 2.3 copy.89
  136.4 37.4 %cosine_multiply_fusion = (f32[1,512,2,2048]{3,1,0,2:T(8,128)}, f32[1,512,2,2048]{3,1,0,2:T(8,128)}) fusion(s32[512,2]{0,1:T(2,128)S(1)} %pad_add_fusion), kind=kLoop, calls=%fused_computation.26 | loop fusion | flops 35651584 | bytes 16781312 | tf_op jit(solution)/shard_map/mul | solution.py:48
  173.7 3.8 copy.86
  177.6 10.0 %reshape.241 = f32[512,8,2,2,32]{4,3,2,1,0:T(2,128)} reshape(f32[32,16,8,128]{3,2,1,0:T(8,128)} %copy.86) | data formatting | bytes 4194304 | tf_op jit(solution)/shard_map/reshape | solution.py:108
  187.5 5.6 %broadcast_multiply_fusion = f32[512,8,2,2,32]{4,3,2,1,0:T(2,128)S(1)} fusion(f32[512,8,2,2,32]{4,3,2,1,0:T(2,128)} %reshape.241, f32[512,2]{1,0:T(8,128)S(1)} %copy.87), kind=kLoop, calls=%fused_computation.31 | loop fusion | flops 524288 | bytes 4198400 | tf_op jit(solution)/shard_map/mul | solution.py:108
  193.2 73.6 %fusion.33 = f32[8,32,2048]{2,1,0:T(8,128)S(1)} fusion(f32[512,8,2,2,32]{4,3,2,1,0:T(2,128)S(1)} %broadcast_multiply_fusion, f32[1,512,2,2048]{3,1,0,2:T(8,128)} %get-tuple-element.39, f32[1,512,2,2048]{3,1,0,2:T(8,128)} %get-tuple-element.38), kind=kOutput, calls=%fused_computation.53 | convolution fusion | flops 12889096192 | bytes 20971520 | tf_op jit(solution)/shard_map/sjhpc,pshi->jci/dot_general | solution.py:110
  267.2 1.4 pad_maximum_fusion.7
  268.6 2.8 collective-permute-start
  271.4 4.0 collective-permute-start.1
  275.4 0.6 compare_and_fusion.1
  276.6 14.4 %collective-permute-done = f32[14,2,3,2048]{3,0,2,1:T(8,128)S(1)} collective-permute-done((f32[14,2,3,2048]{3,0,2,1:T(8,128)}, f32[14,2,3,2048]{3,0,2,1:T(8,128)S(1)}, u32[]{:S(2)}, u32[]{:S(2)}) %collective-permute-start) | collective-permute-done | bytes 688160 | tf_op jit(solution)/shard_map/ppermute | solution.py:30
  291.0 1.1 collective-permute-done.1
  292.1 1.8 pad_maximum_fusion.9
  294.3 0.9 slice.298
  295.2 0.7 slice.297
  295.8 0.6 slice.299
  297.5 1.6 pad_maximum_fusion
  299.2 0.9 slice.273
  300.0 2.4 fusion.30
  303.1 0.9 fusion.24
  304.0 1.5 fusion.27
  305.5 0.7 slice.286
  307.0 0.9 fusion.41
  308.2 0.7 fusion.32
  308.9 1.6 fusion.40
  310.6 0.6 slice.300
  311.7 0.6 fusion.49
  313.2 0.8 copy-done.1
  314.0 2.2 fusion.48
  316.2 1.6 fusion.80
  318.4 17.4 %fusion.57 = f32[512,8,2,2,32]{0,4,1,2,3:T(8,128)S(1)} fusion(f32[8,8,2048]{2,1,0:T(8,128)S(1)} %get-tuple-element.25, f32[8,8,2048]{2,1,0:T(8,128)S(1)} %get-tuple-element.26, f32[8,8,2048]{2,1,0:T(8,128)S(1)} %get-tuple-element.27, f32[8,8,2048]{2,1,0:T(8,128)S(1)} %get-tuple-element.24, f32[1,512,2,2048]{3,1,0,2:T(8,128)} %get-tuple-element.39, ...), kind=kOutput, calls=%fused_computation.86 | convolution fusion | flops 12890669056 | bytes 20971520 | tf_op jit(solution)/shard_map/jci,pshi->sjhpc/dot_general | solution.py:150
  335.7 1.6 copy.109
  337.3 2.9 copy.110
  340.3 8.7 %all-to-all-start.1 = ((f32[512,8,128]{2,1,0:T(8,128)}), f32[512,8,128]{2,1,0:T(8,128)}, u32[]{:S(2)}, u32[]{:S(2)}) async-start(f32[512,8,128]{2,1,0:T(8,128)} %copy.110), calls=%async_computation.1 | async-start | bytes 4194304 | tf_op jit(solution)/shard_map/all_to_all | solution.py:153
  349.1 28.2 %all-to-all-done.1 = f32[512,8,128]{2,1,0:T(8,128)} async-done(((f32[512,8,128]{2,1,0:T(8,128)}), f32[512,8,128]{2,1,0:T(8,128)}, u32[]{:S(2)}, u32[]{:S(2)}) %all-to-all-start.1) | async-done | bytes 2097184 | tf_op jit(solution)/shard_map/all_to_all | solution.py:153
  377.3 21.9 %fusion.20 = f32[1056,16,128]{2,0,1:T(8,128)S(1)} fusion(f32[16,1056,1,256]{3,2,1,0:T(1,128)} %param.7, f32[16,32,8,128]{3,2,0,1:T(8,128)} %bitcast.30, f32[256]{0:T(256)S(1)} %bitcast.93), kind=kOutput, calls=%fused_computation.30 | convolution fusion | flops 6644301824 | bytes 28050432 | tf_op jit(solution)/shard_map/srl,slc->rsc/dot_general | solution.py:156
  399.2 9.5 %fusion.8 = f32[1056,16,64]{2,0,1:T(8,128)} fusion(f32[1056,16,128]{2,0,1:T(8,128)S(1)} %fusion.20, pred[1056,16]{0,1:T(8,128)(4,1)S(1)} %get-tuple-element.41, pred[1056,16]{0,1:T(8,128)(4,1)S(1)} %get-tuple-element.40), kind=kLoop, calls=%fused_computation.13 | loop fusion | flops 3244032 | bytes 13009920 | tf_op jit(solution)/shard_map/add | solution.py:159
  408.7 2.1 copy.113
  410.8 78.7 %reduce-scatter.2.cloned.1.call-done = f32[264,16,64]{2,0,1:T(8,128)} async-done(((f32[1056,16,64]{2,0,1:T(8,128)}), f32[264,16,64]{2,0,1:T(8,128)}) %reduce-scatter.2.cloned.1.call-update) | async-done | bytes 1081360 | tf_op jit(solution)/shard_map/reduce_scatter | solution.py:158
  489.5 3.0 copy.112
  (83 shorter events, 7.2 us)
Async XLA Ops:
  7.2 309.0 %copy-start = (f32[12,2]{0,1:T(2,128)S(1)}, f32[12,2]{0,1:T(2,128)}, u32[]{:S(2)}) copy-start(f32[12,2]{0,1:T(2,128)} %param.11) | copy-start | bytes 292
  7.2 71.1 %all-gather.3.cloned.1.call-start = ((), (), s32[]{:S(2)}) async-start(), calls=%async_computation.4 | async-start | bytes 7864320 | tf_op jit(solution)/shard_map/all_gather | solution.py:92
  8.7 0.5 copy-start.10
  9.2 0.6 copy-start.7
  125.5 8.3 %copy-start.9 = (s32[512]{0:T(512)S(1)}, s32[512]{0:T(512)}, u32[]{:S(2)}) copy-start(s32[512]{0:T(512)} %param.9) | copy-start | bytes 6148
  125.5 48.2 %all-to-all-start = ((f32[16,256,128]{2,0,1:T(8,128)}), f32[16,256,128]{2,0,1:T(8,128)}, u32[]{:S(2)}, u32[]{:S(2)}) async-start(f32[16,256,128]{2,0,1:T(8,128)} %copy.84), calls=%async_computation | async-start | bytes 4194304 | tf_op jit(solution)/shard_map/all_to_all | solution.py:104
  266.8 1.8 copy-start.2
  268.6 22.4 %collective-permute-start = (f32[14,2,3,2048]{3,0,2,1:T(8,128)}, f32[14,2,3,2048]{3,0,2,1:T(8,128)S(1)}, u32[]{:S(2)}, u32[]{:S(2)}) collective-permute-start(f32[14,2,3,2048]{3,0,2,1:T(8,128)} %get-tuple-element.22), channel_id=1, source_target_pairs={{0,1},{1,2},{2,3},{3,4},{4,5},{5,6},{6,7},{7,8},{8,9},{9,10},{10,1... | collective-permute-start | bytes 2064392 | tf_op jit(solution)/shard_map/ppermute | solution.py:30
  271.4 20.7 %collective-permute-start.1 = (f32[14,2,3,2048]{3,0,2,1:T(8,128)}, f32[14,2,3,2048]{3,0,2,1:T(8,128)}, u32[]{:S(2)}, u32[]{:S(2)}) collective-permute-start(f32[14,2,3,2048]{3,0,2,1:T(8,128)} %get-tuple-element.23), channel_id=1, source_target_pairs={{1,0},{2,1},{3,2},{4,3},{5,4},{6,5},{7,6},{8,7},{9,8},{10,9},{11,1... | collective-permute-start | bytes 2064392 | tf_op jit(solution)/shard_map/ppermute | solution.py:31
  307.0 1.2 copy-start.14
  310.5 0.9 copy-start.4
  310.6 1.0 copy-start.6
  310.6 1.0 copy-start.5
  311.7 0.9 copy-start.13
  312.6 1.4 copy-start.1
  313.2 5.1 %slice-start = ((s8[8388608]{0:T(1024)(128)(4,1)}), s8[4194304]{0:T(1024)(128)(4,1)S(1)}, s32[]{:S(2)}) async-start(s8[8388608]{0:T(1024)(128)(4,1)} %bitcast.83), calls=%async_computation.5 | async-start | bytes 8388608
  314.0 4.3 slice-start.1
  316.2 1.8 copy-start.3
  340.3 8.8 %copy-start.8 = (pred[1056]{0:T(1024)(128)(4,1)S(1)}, pred[1056]{0:T(1024)(128)(4,1)}, u32[]{:S(2)}) copy-start(pred[1056]{0:T(1024)(128)(4,1)} %copy-done.7) | copy-start | bytes 3172
  340.3 8.8 %copy-start.11 = (s32[16]{0:T(128)S(1)}, s32[16]{0:T(128)}, u32[]{:S(2)}) copy-start(s32[16]{0:T(128)} %copy-done.10) | copy-start | bytes 196
  340.3 37.1 %copy-start.12 = (f32[1,256]{1,0:T(1,128)S(1)}, f32[1,256]{1,0:T(1,128)}, u32[]{:S(2)}) copy-start(f32[1,256]{1,0:T(1,128)} %param.8) | copy-start | bytes 3076
  340.3 37.1 %all-to-all-start.1 = ((f32[512,8,128]{2,1,0:T(8,128)}), f32[512,8,128]{2,1,0:T(8,128)}, u32[]{:S(2)}, u32[]{:S(2)}) async-start(f32[512,8,128]{2,1,0:T(8,128)} %copy.110), calls=%async_computation.1 | async-start | bytes 4194304 | tf_op jit(solution)/shard_map/all_to_all | solution.py:153
  349.0 140.5 %reduce-scatter.2.cloned.1.call-start = ((), (), s32[]{:S(2)}) async-start(), calls=%async_computation.3 | async-start | bytes 10813440 | tf_op jit(solution)/shard_map/reduce_scatter | solution.py:158
Sparse Core Ops, SparseCore 0:
  9.7 68.6 all-gather.2
  408.9 80.5 reduce-scatter.1
